TPU v7x, 32 devices: a whole 2x2x4 slice. The times are simulated.
32 devices in a mesh: tp: 4 (over z), pp: 8 (over y, x, core).
Axes of the slice: x: 2, y: 2, z: 4, core: 2. Of those that a mesh axis runs over, the one named last changes fastest.
Arguments:
- tokens: bfloat16 [8192, 8192], P('pp', 'tp'), may hold values from -60 to 60
- norm_gain: bfloat16 [8192], P('tp'), may hold values from 0.099609375 to 1.8984375
- weights_gen: bfloat16 [8, 1280, 8192], P('tp', None, 'pp'), may hold values from -2 to 2
- segment_ids: int32 [8, 1024], P('pp'), may hold values from 0 to 15, never falling along the last dimension, each value on 1 to 512 neighbouring positions
Outputs:
- weights_rows: bfloat16 [8, 1280, 8192], P('tp', 'pp')
- attended: bfloat16 [8192, 8192], P('pp', 'tp')
Inputs may be any that keep to these rules, and one draw needn't show every extreme that they name: `segment_ids`: ids never fall along a block; every sequence has 1 to 512 tokens and lies in one block.
All inputs are finite; a program needn't handle non-finite values.
Results may differ from a plain program's by a relative error of at most 0.0075.
Values may be sent and summed in bfloat16 or wider, within the bound.
No kernel may reach another device: no remote copies, remote signals or barrier semaphores. Data moves between devices by JAX's collectives and lax.ppermute only.
A program may use at most 192 MiB of HBM per device.

v0:
```python
import math
import jax
import jax.numpy as jnp
from jax import lax
from jax.sharding import PartitionSpec as P

DH = 128
GROUP = 8
rope_base = 500000.0


def rotary(values, positions):
    half = values.shape[-1] // 2
    freq = jnp.exp(
        jnp.arange(half, dtype=jnp.float32) * (-2.0 * math.log(rope_base) / values.shape[-1])
    )
    angle = positions.astype(jnp.float32)[:, None] * freq[None, :]
    cosine = jnp.cos(angle)
    sine = jnp.sin(angle)
    extra = values.ndim - 2
    cosine = cosine.reshape(cosine.shape[:1] + (1,) * extra + cosine.shape[1:])
    sine = sine.reshape(sine.shape[:1] + (1,) * extra + sine.shape[1:])
    first = values[..., :half]
    second = values[..., half:]
    return jnp.concatenate(
        [first * cosine - second * sine, second * cosine + first * sine], axis=-1
    )


def shards(tokens, norm_gain, weights_gen, segment_ids):
    weights_rows = lax.all_to_all(weights_gen, "pp", split_axis=1, concat_axis=2, tiled=True)
    gathered, gain = (
        lax.all_gather(tokens, "tp", axis=1, tiled=True),
        lax.all_gather(norm_gain, "tp", axis=0, tiled=True),
    )
    floats = gathered.astype(jnp.float32)
    square = jnp.mean(floats * floats, axis=-1, keepdims=True)
    normed = (floats * lax.rsqrt(square + 1e-05) * gain.astype(jnp.float32)).astype(jnp.bfloat16)
    count = normed.shape[0]
    groups = weights_gen.shape[0]
    mixed = jnp.einsum(
        "td,grd->tgr",
        normed,
        lax.all_gather(weights_rows, "pp", axis=1, tiled=True),
        preferred_element_type=jnp.float32,
    )
    mixed = mixed.reshape(count, groups, GROUP + 2, DH)
    seg = segment_ids[0]
    order = jnp.arange(count, dtype=jnp.int32)
    start_index = jnp.sum((seg[None, :] < seg[:, None]).astype(jnp.int32), axis=1)
    positions = order - start_index
    query = rotary(mixed[:, :, :GROUP, :], positions).astype(jnp.bfloat16)
    key_heads = rotary(mixed[:, :, GROUP, :], positions).astype(jnp.bfloat16)
    value_heads = mixed[:, :, GROUP + 1, :].astype(jnp.bfloat16)
    score = jnp.einsum("tgjd,sgd->gjts", query, key_heads, preferred_element_type=jnp.float32) * (
        1.0 / math.sqrt(DH)
    )
    allowed = (seg[:, None] == seg[None, :]) & (order[:, None] >= order[None, :])
    score = jnp.where(allowed[None, None], score, -1e30)
    top = jnp.max(score, axis=-1, keepdims=True)
    expo = jnp.where(allowed[None, None], jnp.exp(score - top), 0.0)
    prob = (expo / jnp.sum(expo, axis=-1, keepdims=True)).astype(jnp.bfloat16)
    output = jnp.einsum("gjts,sgd->tgjd", prob, value_heads, preferred_element_type=jnp.float32)
    attended = output.astype(jnp.bfloat16).reshape(count, groups * GROUP * DH)
    return (weights_rows, attended)


def solution(mesh):
    in_specs = (P("pp", "tp"), P("tp"), P("tp", None, "pp"), P("pp", None))
    out_specs = (P("tp", "pp", None), P("pp", "tp"))
    return jax.shard_map(shards, mesh=mesh, in_specs=in_specs, out_specs=out_specs, check_vma=False)
```

profile of v0, /device:TPU:0, one launch (start us, length us, event | category | flops | bytes accessed | tf_op | source)
XLA Modules:
  0.0 658.1 jit_solution(8889944450149644430)
XLA Ops:
  7.2 0.0 all-gather.3.cloned.1.call-start
  7.2 0.7 all-gather.3.cloned.1.call-update
  7.9 0.0 all-gather.5.cloned.1.call-start
  7.9 9.4 %copy.21 = bf16[2,1280,1024]{2,0,1:T(2,128)(2,1)S(1)} copy(bf16[2,1280,1024]{2,1,0:T(8,128)(2,1)} %param.6) | data formatting | bytes 10485760 | tf_op args[2]
  17.4 65.3 %all_to_all.18 = bf16[2,1280,1024]{2,0,1:T(2,128)(2,1)S(1)} all-to-all(bf16[2,1280,1024]{2,0,1:T(2,128)(2,1)S(1)} %copy.21), channel_id=1, replica_groups=mesh['tp'=4,'pp'=8] {'pp'}, dimensions={1} | all-to-all | bytes 10485760 | tf_op jit(solution)/shard_map/all_to_all | solution.py:31
  82.6 5.2 copy.43
  87.8 0.0 copy-start.2
  87.8 0.0 copy-start.1
  87.8 8.9 %all_to_all.16 = bf16[2,160,8192]{2,1,0:T(8,128)(2,1)} reshape(bf16[2,160,8,1024]{3,2,1,0:T(8,128)(2,1)} %bitcast.49) | data formatting | bytes 10485760 | tf_op jit(solution)/shard_map/all_to_all | solution.py:31
  96.8 0.0 all-gather.5.cloned.1.call-update
  96.8 0.0 copy-done.2
  96.8 24.4 %all_gather.10 = bf16[8192]{0:T(1024)(128)(2,1)S(1)} all-gather(bf16[2048]{0:T(1024)(128)(2,1)S(1)} %copy-done.2), channel_id=1, replica_groups=mesh['tp'=4,'pp'=8] {'tp'}, dimensions={0}, use_global_device_ids=true | all-gather | bytes 20480 | tf_op jit(solution)/shard_map/all_gather | solution.py:34
  121.2 0.0 copy-done.1
  121.2 0.5 convert_reduce_fusion
  121.7 1.9 multiply_cosine_fusion
  123.6 1.6 fusion.16
  125.1 174.1 %all-gather.3.cloned.1.call-done = bf16[1024,8192]{1,0:T(8,128)(2,1)} async-done(((bf16[1024,2048]{1,0:T(8,128)(2,1)}), bf16[1024,8192]{1,0:T(8,128)(2,1)}) %all-gather.3.cloned.1.call-update) | async-done | bytes 16777232 | tf_op jit(solution)/shard_map/all_gather | solution.py:33
  299.3 7.2 %fusion.2 = f32[1024]{0:T(1024)S(1)} fusion(bf16[1024,8192]{1,0:T(8,128)(2,1)} %all-gather.3.cloned.1.call-done), kind=kLoop, calls=%fused_computation.7 | loop fusion | flops 25164800 | bytes 16781312 | tf_op jit(solution)/shard_map/reduce_sum | solution.py:37
  306.5 189.8 %all-gather.5.cloned.1.call-done = bf16[2,1280,8192]{2,1,0:T(8,128)(2,1)} async-done(((bf16[2,160,8192]{2,1,0:T(8,128)(2,1)}), bf16[2,1280,8192]{2,1,0:T(8,128)(2,1)}) %all-gather.5.cloned.1.call-update) | async-done | bytes 41943056 | tf_op jit(solution)/shard_map/all_gather | solution.py:44
  496.3 54.2 %fusion.10 = f32[1024,2,1280]{0,2,1:T(8,128)} fusion(bf16[2,1280,8192]{2,1,0:T(8,128)(2,1)} %all-gather.5.cloned.1.call-done, bf16[1024,8192]{1,0:T(8,128)(2,1)} %all-gather.3.cloned.1.call-done, f32[8192]{0:T(1024)S(1)} %convert_element_type.36, f32[1024]{0:T(1024)S(1)} %add_rsqrt_fusion), kind=kOutput, calls=%fused_computation.15 | convolution fusion | flops 42983227392 | bytes 69242880 | tf_op jit(solution)/shard_map/td,grd->tgr/dot_general | solution.py:41
  550.5 1.3 slice.29
  551.8 8.5 %fusion.27 = (f32[1024,2,8,64]{0,3,2,1:T(8,128)}, f32[1024,2,8,64]{0,3,2,1:T(8,128)}) fusion(f32[1024,2,10,128]{0,3,2,1:T(8,128)} %bitcast.52), kind=kLoop, calls=%fused_computation.42 | loop fusion | bytes 16777216 | tf_op jit(solution)/shard_map/slice | solution.py:24
  560.2 0.3 copy.34
  560.5 6.9 %copy.36 = f32[1024,2,8,64]{3,0,2,1:T(8,128)} copy(f32[1024,2,8,64]{0,3,2,1:T(8,128)} %get-tuple-element.10) | data formatting | bytes 8388608
  567.5 6.9 %copy.35 = f32[1024,2,8,64]{3,0,2,1:T(8,128)} copy(f32[1024,2,8,64]{0,3,2,1:T(8,128)} %get-tuple-element.11) | data formatting | bytes 8388608
  574.3 0.4 subtract_convert_fusion.1
  574.7 0.0 copy-start
  574.8 9.6 %subtract_convert_fusion = (bf16[1024,2,8,64]{3,0,2,1:T(8,128)(2,1)}, bf16[1024,2,8,64]{3,0,2,1:T(8,128)(2,1)}) fusion(f32[1024,2,8,64]{3,0,2,1:T(8,128)} %copy.36, f32[1024,2,8,64]{3,0,2,1:T(8,128)} %copy.35, f32[1024,64]{1,0:T(8,128)S(1)} %get-tuple-element.15, f32[1024,64]{1,0:T(8,128)S(1)} %get-tuple-element.14), kind=kLoop, calls=%fused_computation.19 | loop fusion | flops 8388608 | bytes 13107200 | tf_op jit(solution)/shard_map/convert
  584.4 0.0 copy-done
  584.4 36.3 %fusion.28 = (f32[2,8,1024]{2,1,0:T(8,128)S(1)}, f32[2,8,1024,1024]{2,3,1,0:T(8,128)}) fusion(pred[1024,1024]{0,1:T(8,128)(4,1)S(1)} %copy-done, bf16[1024,2,8,64]{3,0,2,1:T(8,128)(2,1)} %get-tuple-element.9, bf16[1024,2,8,64]{3,0,2,1:T(8,128)(2,1)} %get-tuple-element.8, bf16[1024,2,64]{2,0,1:T(8,128)(2,1)S(1)} %get-tuple-element.13, ...), kind=kOutput, calls=%fused_computation.43 | convolution fusion | flops 4388291584 | bytes 72941568 | tf_op jit(solution)/shard_map/sub | solution.py:61
  620.7 24.1 %fusion.17 = bf16[2,128,8,1024]{3,1,2,0:T(8,128)(2,1)} fusion(f32[2,8,1024,1024]{2,3,1,0:T(8,128)} %get-tuple-element.17, f32[2,8,1024]{2,1,0:T(8,128)S(1)} %get-tuple-element.16, f32[1024,2,10,128]{0,3,2,1:T(8,128)} %bitcast.53), kind=kOutput, calls=%fused_computation.26 | convolution fusion | flops 4330618880 | bytes 71892992 | tf_op jit(solution)/shard_map/gjts,sgd->tgjd/dot_general | solution.py:63
  644.8 6.4 copy.29
  (4 shorter events, 0.0 us)
Async XLA Ops:
  7.2 292.1 %all-gather.3.cloned.1.call-start = ((), (), s32[]{:S(2)}) async-start(), calls=%async_computation.1 | async-start | bytes 20971520 | tf_op jit(solution)/shard_map/all_gather | solution.py:33
  7.9 488.4 %all-gather.5.cloned.1.call-start = ((), (), s32[]{:S(2)}) async-start(), calls=%async_computation.2 | async-start | bytes 47185920 | tf_op jit(solution)/shard_map/all_gather | solution.py:44
  87.8 8.9 %copy-start.2 = (bf16[2048]{0:T(1024)(128)(2,1)S(1)}, bf16[2048]{0:T(1024)(128)(2,1)}, u32[]{:S(2)}) copy-start(bf16[2048]{0:T(1024)(128)(2,1)} %param.5) | copy-start | bytes 12292
  87.8 33.3 %copy-start.1 = (s32[1,1024]{1,0:T(1,128)S(1)}, s32[1,1024]{1,0:T(1,128)}, u32[]{:S(2)}) copy-start(s32[1,1024]{1,0:T(1,128)} %param.7) | copy-start | bytes 12292
  574.7 9.7 %copy-start = (pred[1024,1024]{0,1:T(8,128)(4,1)S(1)}, pred[1024,1024]{0,1:T(8,128)(4,1)}, u32[]{:S(2)}) copy-start(pred[1024,1024]{0,1:T(8,128)(4,1)} %fusion.16) | copy-start | bytes 3145732
Sparse Core Ops, SparseCore 0:
  9.5 289.6 all-gather.2
  301.7 194.4 all-gather.4
where the time goes:
time: 659 us; the launch traced here: 658 us
  waiting for transfers between devices  365 us (55%)
  matrix products  115 us (17%)
  blocking collectives  89.6 us (14%)
  local copies, waits for them, and re-layouts  53.8 us (8%)
  other arithmetic  21.2 us (3%)
  between operations  14.1 us (2%)
    all_gather x1, waiting for transfers between devices, shards(): lax.all_gather(weights_rows, 'pp', axis=1, tiled=True)  190 us
    all_gather x1, waiting for transfers between devices, shards(): lax.all_gather(tokens, 'tp', axis=1, tiled=True)  174 us
    all_to_all x1, blocking collectives, shards(): lax.all_to_all(weights_gen, 'pp', split_axis=1, concat_axis=2, tiled=True)  65.3 us
    dot_general x1, matrix products, shards(): jnp.einsum('td,grd->tgr', normed, lax.all_gather(weights_rows, 'pp', axis...  54.2 us
    sub x1, matrix products, shards(): expo = jnp.where(allowed[None, None], jnp.exp(score - top), 0.0)  36.3 us
    unnamed x11, local copies, waits for them, and re-layouts  29.9 us
    all_gather x1, blocking collectives, shards(): lax.all_gather(norm_gain, 'tp', axis=0, tiled=True)  24.4 us
    dot_general x1, matrix products, shards(): jnp.einsum('gjts,sgd->tgjd', prob, value_heads, preferred_element_type=jn...  24.1 us
  transfers between devices with their start and end apart: 2, of which 2 were waited for; matrix products, arithmetic and copies ran while one was open for 4% of the time, Pallas kernels for 0%

commit v1 on v0

--- a/solution.py
+++ b/solution.py
@@ -41,7 +41,7 @@
     mixed = jnp.einsum(
         "td,grd->tgr",
         normed,
-        lax.all_gather(weights_rows, "pp", axis=1, tiled=True),
+        jnp.concatenate(jax.lax.all_gather(weights_rows, "pp"), 1),
         preferred_element_type=jnp.float32,
     )
     mixed = mixed.reshape(count, groups, GROUP + 2, DH)

time: 659 us -> 631 us (0.958)
  local copies, waits for them, and re-layouts: 53.8 us -> 40.3 us
  waiting for transfers between devices: 365 us -> 356 us
    unnamed x11 -> x6, local copies, waits for them, and re-layouts: 29.9 us -> 15.8 us
    slice x2 -> x0, local copies, waits for them, and re-layouts: 9.75 us -> none  [the longest x1 8.45 us: rotary(): second = values[..., half:]]
    all_gather x0 -> x1, local copies, waits for them, and re-layouts: none -> 8.95 us  [shards(): jax.lax.all_gather(weights_rows, 'pp')]
    all_gather x1, waiting for transfers between devices: 174 us -> 166 us  [shards(): lax.all_gather(tokens, 'tp', axis=1, tiled=True)]
where the time goes in v1:
time: 631 us; the launch traced here: 630 us
  waiting for transfers between devices  356 us (56%)
  matrix products  113 us (18%)
  blocking collectives  89.5 us (14%)
  local copies, waits for them, and re-layouts  40.3 us (6%)
  other arithmetic  16.6 us (3%)
  between operations  14.1 us (2%)
    all_gather x1, waiting for transfers between devices, shards(): jax.lax.all_gather(weights_rows, 'pp')  189 us
    all_gather x1, waiting for transfers between devices, shards(): lax.all_gather(tokens, 'tp', axis=1, tiled=True)  166 us
    all_to_all x1, blocking collectives, shards(): lax.all_to_all(weights_gen, 'pp', split_axis=1, concat_axis=2, tiled=True)  65.3 us
    dot_general x1, matrix products, shards(): jnp.einsum('td,grd->tgr', normed, jnp.concatenate(jax.lax.all_gather(weig...  54.2 us
    sub x1, matrix products, shards(): expo = jnp.where(allowed[None, None], jnp.exp(score - top), 0.0)  35.1 us
    all_gather x1, blocking collectives, shards(): lax.all_gather(norm_gain, 'tp', axis=0, tiled=True)  24.3 us
    dot_general x1, matrix products, shards(): jnp.einsum('gjts,sgd->tgjd', prob, value_heads, preferred_element_type=jn...  24.2 us
    unnamed x6, local copies, waits for them, and re-layouts  15.8 us
  transfers between devices with their start and end apart: 2, of which 2 were waited for; matrix products, arithmetic and copies ran while one was open for 4% of the time, Pallas kernels for 0%

profile of v1, /device:TPU:0, one launch (start us, length us, event | category | flops | bytes accessed | tf_op | source)
XLA Modules:
  0.0 630.1 jit_solution(5889430536191746193)
XLA Ops:
  7.2 0.0 all-gather.3.cloned.1.call-start
  7.2 0.7 all-gather.3.cloned.1.call-update
  7.9 0.0 all-gather.5.cloned.1.call-start
  7.9 9.4 %copy.11 = bf16[2,1280,1024]{2,0,1:T(2,128)(2,1)S(1)} copy(bf16[2,1280,1024]{2,1,0:T(8,128)(2,1)} %param.6) | data formatting | bytes 10485760 | tf_op args[2]
  17.4 65.3 %all_to_all.18 = bf16[2,1280,1024]{2,0,1:T(2,128)(2,1)S(1)} all-to-all(bf16[2,1280,1024]{2,0,1:T(2,128)(2,1)S(1)} %copy.11), channel_id=1, replica_groups=mesh['tp'=4,'pp'=8] {'pp'}, dimensions={1} | all-to-all | bytes 10485760 | tf_op jit(solution)/shard_map/all_to_all | solution.py:31
  82.6 5.3 copy.12
  87.9 0.0 copy-start.1
  87.9 0.0 copy-start
  87.9 9.0 %all_gather.14 = bf16[1,2,160,8192]{3,2,0,1:T(8,128)(2,1)} reshape(bf16[2,160,8,1024]{3,2,1,0:T(8,128)(2,1)} %copy.12) | data formatting | bytes 10485760 | tf_op jit(solution)/shard_map/all_gather | solution.py:44
  96.8 0.0 all-gather.5.cloned.1.call-update
  96.9 0.0 copy-done.1
  96.9 24.3 %all_gather.13 = bf16[8192]{0:T(1024)(128)(2,1)S(1)} all-gather(bf16[2048]{0:T(1024)(128)(2,1)S(1)} %copy-done.1), channel_id=1, replica_groups=mesh['tp'=4,'pp'=8] {'tp'}, dimensions={0}, use_global_device_ids=true | all-gather | bytes 20480 | tf_op jit(solution)/shard_map/all_gather | solution.py:34
  121.2 0.0 copy-done
  121.2 0.5 convert_reduce_fusion
  121.7 1.0 multiply_cosine_fusion
  122.7 1.6 fusion.16
  124.2 8.9 %all_to_all.16 = bf16[2,160,8192]{2,1,0:T(8,128)(2,1)} reshape(bf16[2,160,8,1024]{3,2,1,0:T(8,128)(2,1)} %copy.12) | data formatting | bytes 10485760 | tf_op jit(solution)/shard_map/all_to_all | solution.py:31
  133.2 166.1 %all-gather.3.cloned.1.call-done = bf16[1024,8192]{1,0:T(8,128)(2,1)} async-done(((bf16[1024,2048]{1,0:T(8,128)(2,1)}), bf16[1024,8192]{1,0:T(8,128)(2,1)}) %all-gather.3.cloned.1.call-update) | async-done | bytes 16777232 | tf_op jit(solution)/shard_map/all_gather | solution.py:33
  299.3 7.2 %fusion.2 = f32[1024]{0:T(1024)S(1)} fusion(bf16[1024,8192]{1,0:T(8,128)(2,1)} %all-gather.3.cloned.1.call-done), kind=kLoop, calls=%fused_computation.7 | loop fusion | flops 25164800 | bytes 16781312 | tf_op jit(solution)/shard_map/reduce_sum | solution.py:37
  306.5 189.2 %all-gather.5.cloned.1.call-done = bf16[8,2,160,8192]{3,2,0,1:T(8,128)(2,1)} async-done(((bf16[1,2,160,8192]{3,2,0,1:T(8,128)(2,1)}), bf16[8,2,160,8192]{3,2,0,1:T(8,128)(2,1)}) %all-gather.5.cloned.1.call-update) | async-done | bytes 41943056 | tf_op jit(solution)/shard_map/all_gather | solution.py:44
  495.7 54.2 %fusion.10 = f32[1024,2,10,128]{0,3,2,1:T(8,128)} fusion(bf16[2,10,128,8192]{3,2,1,0:T(8,128)(2,1)} %bitcast.58, bf16[1024,8192]{1,0:T(8,128)(2,1)} %all-gather.3.cloned.1.call-done, f32[8192]{0:T(1024)S(1)} %convert_element_type.36, f32[1024]{0:T(1024)S(1)} %add_rsqrt_fusion), kind=kOutput, calls=%fused_computation.15 | convolution fusion | flops 42983227392 | bytes 69242880 | tf_op jit(solution)/shard_map/td,grd->tgr/dot_general | solution.py:41
  549.9 1.3 slice_bitcast_fusion
  551.2 6.2 subtract_convert_fusion
  557.4 0.2 subtract_convert_fusion.1
  557.6 35.1 %fusion.27 = (f32[2,8,1024]{2,1,0:T(8,128)S(1)}, f32[2,8,1024,1024]{2,3,1,0:T(8,128)}) fusion(pred[1024,1024]{0,1:T(8,128)(4,1)} %fusion.16, bf16[1024,2,8,64]{0,3,2,1:T(8,128)(2,1)} %get-tuple-element.7, bf16[1024,2,8,64]{0,3,2,1:T(8,128)(2,1)S(1)} %get-tuple-element.6, bf16[1024,2,64]{0,2,1:T(8,128)(2,1)S(1)} %get-tuple-element.9, ...), kind=kOutput, calls=%fused_computation.42 | convolution fusion | flops 4388291584 | bytes 72941568 | tf_op jit(solution)/shard_map/sub | solution.py:61
  592.7 24.2 %fusion.18 = bf16[2,128,8,1024]{3,1,2,0:T(8,128)(2,1)} fusion(f32[2,8,1024,1024]{2,3,1,0:T(8,128)} %get-tuple-element.13, f32[2,8,1024]{2,1,0:T(8,128)S(1)} %get-tuple-element.12, f32[1024,2,10,128]{0,3,2,1:T(8,128)} %fusion.10), kind=kOutput, calls=%fused_computation.26 | convolution fusion | flops 4330618880 | bytes 71892992 | tf_op jit(solution)/shard_map/gjts,sgd->tgjd/dot_general | solution.py:63
  616.8 6.4 %copy.17 = bf16[1024,2048]{1,0:T(8,128)(2,1)} copy(bf16[1024,2048]{0,1:T(8,128)(2,1)} %bitcast.55) | data formatting | bytes 8388608
  (4 shorter events, 0.0 us)
Async XLA Ops:
  7.2 292.1 %all-gather.3.cloned.1.call-start = ((), (), s32[]{:S(2)}) async-start(), calls=%async_computation.1 | async-start | bytes 20971520 | tf_op jit(solution)/shard_map/all_gather | solution.py:33
  7.9 487.8 %all-gather.5.cloned.1.call-start = ((), (), s32[]{:S(2)}) async-start(), calls=%async_computation.2 | async-start | bytes 47185920 | tf_op jit(solution)/shard_map/all_gather | solution.py:44
  87.9 9.0 %copy-start.1 = (bf16[2048]{0:T(1024)(128)(2,1)S(1)}, bf16[2048]{0:T(1024)(128)(2,1)}, u32[]{:S(2)}) copy-start(bf16[2048]{0:T(1024)(128)(2,1)} %param.5) | copy-start | bytes 12292
  87.9 33.3 %copy-start = (s32[1,1024]{1,0:T(1,128)S(1)}, s32[1,1024]{1,0:T(1,128)}, u32[]{:S(2)}) copy-start(s32[1,1024]{1,0:T(1,128)} %param.7) | copy-start | bytes 12292
Sparse Core Ops, SparseCore 0:
  9.5 289.6 all-gather.2
  301.2 194.4 all-gather.4
